TPU v7x, 128 devices: a whole 4x4x4 slice. The times are simulated.
128 devices in a mesh: vocab: 8 (over z, core), sample: 4 (over y), prompt: 4 (over x).
Axes of the slice: x: 4, y: 4, z: 4, core: 2. Of those that a mesh axis runs over, the one named last changes fastest.
Arguments:
- hidden: bfloat16 [1024, 4608], P(('sample', 'prompt'), 'vocab'), may hold values from -12 to 12
- gain: float32 [4608], replicated, may hold values from 0.25 to 1.75
- head: bfloat16 [4608, 256000], P(None, ('vocab', 'sample', 'prompt')), may hold values from -0.25 to 0.25
- candidates: int32 [32, 16], replicated, may hold values from 0 to 255999
- row_prompt: int32 [1024], replicated, may hold values from 0 to 31, as said below
Outputs:
- log_votes: float32 [32, 16], replicated
- row_lse: float32 [1024], P(('sample', 'prompt'))
Inputs may be any that keep to these rules, and one draw needn't show every extreme that they name: `row_prompt`: every prompt has at least one row; the rows of a prompt may stand anywhere among the 1024 rows.
All inputs are finite; a program needn't handle non-finite values.
Results may differ from a plain program's by a relative error of at most 0.00051.
Values may be sent and summed in bfloat16 or wider, within the bound.
No kernel may reach another device: no remote copies, remote signals or barrier semaphores. Data moves between devices by JAX's collectives and lax.ppermute only.
A program may use at most 128 MiB of HBM per device.

v0:
```python
import jax
import jax.numpy as jnp
from jax import lax
from jax.sharding import PartitionSpec as P

CAP = 30.0
EPS = 1e-06


def sent_to_all(array, axis):
    length = lax.axis_size(axis)
    return lax.all_to_all(
        jnp.broadcast_to(array[None], (length, *array.shape)), axis, 0, 0, tiled=True
    )


def over_copies(array, axis):
    return sent_to_all(array, axis).sum(axis=0)


def over_pieces(array, axis):
    parts = lax.all_gather(array, axis)
    return parts.sum(axis=0)


def body(hidden, gain, head, candidates, row_prompt):
    width = head.shape[0]
    vocab_dev = head.shape[1]
    shards = lax.axis_size("vocab")
    row_dev = hidden.shape[0]
    cols = hidden.shape[1]
    prompts = candidates.shape[0]
    xf = hidden.astype(jnp.float32)
    squared = over_copies(jnp.sum(xf * xf, axis=1), "vocab")
    scale = lax.rsqrt(squared / width + EPS)
    gain_part = lax.dynamic_slice_in_dim(gain, lax.axis_index("vocab") * cols, cols)
    normed = (xf * scale[:, None] * gain_part[None, :]).astype(jnp.bfloat16)
    pieces = lax.all_gather(normed[None], ("vocab", "sample", "prompt"), axis=0, tiled=True)
    groups = pieces.shape[0] // shards
    pieces = pieces.reshape(shards, groups, row_dev, cols)
    weight = head.reshape(shards, cols, vocab_dev)
    raw = jnp.einsum("vgrd,vdc->grc", pieces, weight, preferred_element_type=jnp.float32)
    logits = CAP * jnp.tanh(raw.reshape(groups * row_dev, vocab_dev) / CAP)
    rows = logits.shape[0]
    exps = jnp.exp(logits)
    sumexp = jnp.sum(exps, axis=1)
    onehot = (row_prompt[:, None] == jnp.arange(prompts, dtype=jnp.int32)[None, :]).astype(
        jnp.float32
    )
    cands = candidates.shape[1]
    offset = lax.axis_index(("vocab", "sample", "prompt")) * vocab_dev
    cand_local = candidates - offset
    columns = jnp.arange(vocab_dev, dtype=jnp.int32)
    selector = (columns[:, None, None] == cand_local[None, :, :]).astype(jnp.float32)
    selector = selector.reshape(vocab_dev, prompts * cands)
    matched = jnp.dot(
        exps, selector, precision=lax.Precision.HIGHEST, preferred_element_type=jnp.float32
    )
    numer = jnp.einsum(
        "rpc,rp->rc",
        matched.reshape(rows, prompts, cands),
        onehot,
        precision=lax.Precision.HIGHEST,
        preferred_element_type=jnp.float32,
    )
    group = lax.axis_index(("sample", "prompt"))
    totals, numers = (
        over_pieces(sumexp, ("vocab", "sample", "prompt")),
        over_pieces(numer, ("vocab", "sample", "prompt")),
    )
    prob = numers / totals[:, None]
    tally = jnp.dot(
        onehot.T, prob, precision=lax.Precision.HIGHEST, preferred_element_type=jnp.float32
    )
    row_lse = lax.dynamic_slice_in_dim(jnp.log(totals), group * row_dev, row_dev, 0)
    return (jnp.log(tally), row_lse)


def solution(mesh):
    placed = (
        P(("sample", "prompt"), "vocab"),
        P(),
        P(None, ("vocab", "sample", "prompt")),
        P(),
        P(),
    )
    return jax.shard_map(
        body, mesh=mesh, in_specs=placed, out_specs=(P(), P(("sample", "prompt"))), check_vma=False
    )
```

profile of v0, /device:TPU:1, one launch (start us, length us, event | category | flops | bytes accessed | tf_op | source)
XLA Modules:
  0.0 215.8 jit_solution(7561266731137708748)
XLA Ops:
  7.2 1.0 fusion.14
  8.2 0.6 broadcast_in_dim.4
  8.8 6.8 %all-to-all-start = ((f32[8,1,64]{2,1,0:T(1,128)}), f32[8,1,64]{2,1,0:T(1,128)S(1)}, u32[]{:S(2)}, u32[]{:S(2)}) async-start(f32[8,1,64]{2,1,0:T(1,128)} %broadcast_in_dim.4), calls=%async_computation | async-start | bytes 8192 | tf_op jit(solution)/shard_map/all_to_all | solution.py:12
  15.6 0.0 all-gather.6.cloned.1.call-start
  15.6 0.8 dynamic_slice.6
  16.4 3.8 %all-to-all-done = f32[8,1,64]{2,1,0:T(1,128)S(1)} async-done(((f32[8,1,64]{2,1,0:T(1,128)}), f32[8,1,64]{2,1,0:T(1,128)S(1)}, u32[]{:S(2)}, u32[]{:S(2)}) %all-to-all-start) | async-done | bytes 2080 | tf_op jit(solution)/shard_map/all_to_all | solution.py:12
  20.1 1.6 fusion.16
  21.8 0.0 all-gather.6.cloned.1.call-update
  21.8 0.0 copy-start.1
  21.8 0.0 copy-start
  21.8 0.0 all-gather.8.cloned.1.call-start
  21.8 24.8 %copy.23 = bf16[4608,2000]{1,0:T(8,128)(2,1)} copy(bf16[4608,2000]{0,1:T(8,128)(2,1)} %param.7) | data formatting | bytes 36864000 | tf_op args[2]
  46.6 0.0 copy-done.1
  46.6 0.2 fusion.12
  46.8 0.2 copy.33
  47.0 0.0 copy-done
  47.0 46.3 %all-gather.6.cloned.1.call-done = bf16[8192,576]{1,0:T(8,128)(2,1)} async-done(((bf16[64,576]{1,0:T(8,128)(2,1)}), bf16[8192,576]{1,0:T(8,128)(2,1)}) %all-gather.6.cloned.1.call-update) | async-done | bytes 9437200 | tf_op jit(solution)/shard_map/all_gather | solution.py:38
  93.3 27.7 %fusion.5 = (f32[1024]{0:T(1024)S(1)}, f32[1024,2000,1]{0,1,2:T(8,128)S(1)}) fusion(bf16[1024,576,8]{1,0,2:T(8,128)(2,1)} %bitcast.37, bf16[8,576,2000]{2,1,0:T(8,128)(2,1)} %bitcast.34), kind=kOutput, calls=%fused_computation.7 | convolution fusion | flops 18880512000 | bytes 36065280 | tf_op jit(solution)/shard_map/vgrd,vdc->grc/dot_general | solution.py:42
  121.0 9.4 %multiply_reduce_fusion = f32[1024,16]{0,1:T(8,128)} fusion(f32[1024,32]{0,1:T(8,128)S(1)} %copy.33, s32[32,16]{0,1:T(8,128)S(1)} %broadcast_subtract_fusion, f32[1024,2000,1]{0,1,2:T(8,128)S(1)} %get-tuple-element.3), kind=kOutput, calls=%fused_computation.11 | convolution fusion | flops 12589064192 | bytes 8390656 | tf_op jit(solution)/shard_map/dot_general | solution.py:56
  130.4 0.0 all-gather.8.cloned.1.call-update
  130.5 55.7 %all-gather.2 = f32[131072]{0:T(1024)S(1)} all-gather(f32[1024]{0:T(1024)S(1)} %get-tuple-element.2), channel_id=4, replica_groups=mesh['vocab'=8,'sample'=4,'prompt'=4] {'vocab','sample','prompt'}, dimensions={0}, use_global_device_ids=true | all-gather | bytes 528384 | tf_op jit(solution)/shard_map/all_gather | solution.py:22
  186.1 0.1 reshape.42
  186.3 0.6 dynamic_slice.7
  186.9 11.8 %all-gather.8.cloned.1.call-done = f32[131072,16]{0,1:T(8,128)} async-done(((f32[1024,16]{0,1:T(8,128)}), f32[131072,16]{0,1:T(8,128)}) %all-gather.8.cloned.1.call-update) | async-done | bytes 8388624 | tf_op jit(solution)/shard_map/all_gather | solution.py:22
  198.6 8.2 %copy.35 = f32[2,8,128,1024]{3,2,1,0:T(8,128)S(1)} copy(f32[2,8,128,1024]{3,1,2,0:T(8,128)} %bitcast.35) | data formatting | bytes 16777216
  206.9 1.1 bitcast_reduce_fusion
  207.9 1.0 convolution_log_fusion
  (5 shorter events, 0.1 us)
Async XLA Ops:
  8.8 11.3 %all-to-all-start = ((f32[8,1,64]{2,1,0:T(1,128)}), f32[8,1,64]{2,1,0:T(1,128)S(1)}, u32[]{:S(2)}, u32[]{:S(2)}) async-start(f32[8,1,64]{2,1,0:T(1,128)} %broadcast_in_dim.4), calls=%async_computation | async-start | bytes 8192 | tf_op jit(solution)/shard_map/all_to_all | solution.py:12
  15.6 77.7 %all-gather.6.cloned.1.call-start = ((), (), s32[]{:S(2)}) async-start(), calls=%async_computation.1 | async-start | bytes 10567680 | tf_op jit(solution)/shard_map/all_gather | solution.py:38
  21.8 24.9 %copy-start.1 = (s32[1024]{0:T(1024)S(1)}, s32[1024]{0:T(1024)}, u32[]{:S(2)}) copy-start(s32[1024]{0:T(1024)} %param.9) | copy-start | bytes 12292
  21.8 25.2 %copy-start = (s32[32,16]{0,1:T(8,128)S(1)}, s32[32,16]{0,1:T(8,128)}, u32[]{:S(2)}) copy-start(s32[32,16]{0,1:T(8,128)} %param.8) | copy-start | bytes 6148
  21.8 176.8 %all-gather.8.cloned.1.call-start = ((), (), s32[]{:S(2)}) async-start(), calls=%async_computation.2 | async-start | bytes 8454144 | tf_op jit(solution)/shard_map/all_gather | solution.py:22
Sparse Core Ops, SparseCore 0:
  21.9 71.3 all-gather.5
  130.6 68.0 all-gather.7
where the time goes:
time: 217 us; the launch traced here: 216 us
  waiting for transfers between devices  61.8 us (28%)
  blocking collectives  55.7 us (26%)
  matrix products  38.1 us (18%)
  local copies, waits for them, and re-layouts  35.3 us (16%)
  between operations  14.1 us (6%)
  starting transfers between devices  6.85 us (3%)
  other arithmetic  3.95 us (2%)
    all_gather x1, blocking collectives, over_pieces(): parts = lax.all_gather(array, axis)  55.7 us
    all_gather x1, waiting for transfers between devices, body(): lax.all_gather(normed[None], ('vocab', 'sample', 'prompt'), axis=0, tiled...  46.3 us
    unnamed x7, local copies, waits for them, and re-layouts  33.2 us
    dot_general x1, matrix products, body(): jnp.einsum('vgrd,vdc->grc', pieces, weight, preferred_element_type=jnp.fl...  27.7 us
    all_gather x1, waiting for transfers between devices, over_pieces(): parts = lax.all_gather(array, axis)  11.8 us
    dot_general x1, matrix products, body(): jnp.dot(exps, selector, precision=lax.Precision.HIGHEST, preferred_elemen...  9.41 us
    all_to_all x1, starting transfers between devices, sent_to_all(): lax.all_to_all(jnp.broadcast_to(array[None], (length, *array.shape)), axi...  6.8 us
  transfers between devices with their start and end apart: 3, of which 3 were waited for; matrix products, arithmetic and copies ran while one was open for 12% of the time, Pallas kernels for 0%

commit v1 on v0

--- a/solution.py
+++ b/solution.py
@@ -35,7 +35,15 @@
     scale = lax.rsqrt(squared / width + EPS)
     gain_part = lax.dynamic_slice_in_dim(gain, lax.axis_index("vocab") * cols, cols)
     normed = (xf * scale[:, None] * gain_part[None, :]).astype(jnp.bfloat16)
-    pieces = lax.all_gather(normed[None], ("vocab", "sample", "prompt"), axis=0, tiled=True)
+    pieces = jnp.concatenate(
+        lax.all_to_all(
+            jnp.stack([normed[None]] * lax.axis_size(("vocab", "sample", "prompt"))),
+            ("vocab", "sample", "prompt"),
+            0,
+            0,
+        ),
+        axis=0,
+    )
     groups = pieces.shape[0] // shards
     pieces = pieces.reshape(shards, groups, row_dev, cols)
     weight = head.reshape(shards, cols, vocab_dev)

time: 217 us -> 302 us (1.39)
  waiting for transfers between devices: 61.8 us -> 118 us
  blocking collectives: 55.7 us -> 71.2 us
  starting transfers between devices: 6.85 us -> 15.1 us
  local copies, waits for them, and re-layouts: 35.3 us -> 40.7 us
    all_to_all x0 -> x1, waiting for transfers between devices: none -> 98.8 us  [body(): lax.all_to_all(jnp.stack([normed[None]] * lax.axis_size(('vocab', 'sample...]
    all_gather x1 -> x0, waiting for transfers between devices: 46.3 us -> none  [body(): lax.all_gather(normed[None], ('vocab', 'sample', 'prompt'), axis=0, tiled...]
    all_gather x1, blocking collectives: 55.7 us -> 71.2 us  [over_pieces(): parts = lax.all_gather(array, axis)]
    all_to_all x0 -> x1, starting transfers between devices: none -> 8.22 us  [body(): lax.all_to_all(jnp.stack([normed[None]] * lax.axis_size(('vocab', 'sample...]
    another operation x0 -> x1, local copies, waits for them, and re-layouts: none -> 5.45 us  [body(): jnp.stack([normed[None]] * lax.axis_size(('vocab', 'sample', 'prompt')))]
    all_gather x1, waiting for transfers between devices: 11.8 us -> 15.5 us  [over_pieces(): parts = lax.all_gather(array, axis)]
  transfers between devices with their start and end apart: 3 -> 3, of which waited for: 3 -> 3; matrix products, arithmetic and copies ran while one was open for 12% -> 9% of each run, Pallas kernels for 0% -> 0%
where the time goes in v1:
time: 302 us; the launch traced here: 301 us
  waiting for transfers between devices  118 us (39%)
  blocking collectives  71.2 us (24%)
  local copies, waits for them, and re-layouts  40.7 us (13%)
  matrix products  38.1 us (13%)
  starting transfers between devices  15.1 us (5%)
  between operations  14.1 us (5%)
  other arithmetic  3.31 us (1%)
    all_to_all x1, waiting for transfers between devices, body(): lax.all_to_all(jnp.stack([normed[None]] * lax.axis_size(('vocab', 'sample...  98.8 us
    all_gather x1, blocking collectives, over_pieces(): parts = lax.all_gather(array, axis)  71.2 us
    unnamed x7, local copies, waits for them, and re-layouts  33.2 us
    dot_general x1, matrix products, body(): jnp.einsum('vgrd,vdc->grc', pieces, weight, preferred_element_type=jnp.fl...  27.7 us
    all_gather x1, waiting for transfers between devices, over_pieces(): parts = lax.all_gather(array, axis)  15.5 us
    dot_general x1, matrix products, body(): jnp.dot(exps, selector, precision=lax.Precision.HIGHEST, preferred_elemen...  9.38 us
    all_to_all x1, starting transfers between devices, body(): lax.all_to_all(jnp.stack([normed[None]] * lax.axis_size(('vocab', 'sample...  8.22 us
    all_to_all x1, starting transfers between devices, sent_to_all(): lax.all_to_all(jnp.broadcast_to(array[None], (length, *array.shape)), axi...  6.8 us
  transfers between devices with their start and end apart: 3, of which 3 were waited for; matrix products, arithmetic and copies ran while one was open for 9% of the time, Pallas kernels for 0%

profile of v1, /device:TPU:1, one launch (start us, length us, event | category | flops | bytes accessed | tf_op | source)
XLA Modules:
  0.0 300.5 jit_solution(8129218607477149020)
XLA Ops:
  7.2 1.0 fusion.14
  8.2 0.6 broadcast_in_dim.2
  8.8 6.8 %all-to-all-start = ((f32[8,1,64]{2,1,0:T(1,128)}), f32[8,1,64]{2,1,0:T(1,128)S(1)}, u32[]{:S(2)}, u32[]{:S(2)}) async-start(f32[8,1,64]{2,1,0:T(1,128)} %broadcast_in_dim.2), calls=%async_computation | async-start | bytes 8192 | tf_op jit(solution)/shard_map/all_to_all | solution.py:12
  15.6 0.8 dynamic_slice.6
  16.4 3.8 %all-to-all-done = f32[8,1,64]{2,1,0:T(1,128)S(1)} async-done(((f32[8,1,64]{2,1,0:T(1,128)}), f32[8,1,64]{2,1,0:T(1,128)S(1)}, u32[]{:S(2)}, u32[]{:S(2)}) %all-to-all-start) | async-done | bytes 2080 | tf_op jit(solution)/shard_map/all_to_all | solution.py:12
  20.1 1.0 fusion.16
  21.1 5.4 %stack.3 = bf16[128,1,64,576]{3,2,1,0:T(8,128)(2,1)} broadcast(bf16[64,576]{1,0:T(8,128)(2,1)S(1)} %fusion.16), dimensions={2,3} | broadcast | bytes 9510912 | tf_op jit(solution)/shard_map/stack | solution.py:40
  26.6 8.2 %all-to-all-start.1 = ((bf16[128,1,64,576]{3,2,1,0:T(8,128)(2,1)}), bf16[128,1,64,576]{3,2,1,0:T(8,128)(2,1)}, u32[]{:S(2)}, u32[]{:S(2)}) async-start(bf16[128,1,64,576]{3,2,1,0:T(8,128)(2,1)} %stack.3), calls=%async_computation.1 | async-start | bytes 20971520 | tf_op jit(solution)/shard_map/all_to_all | solution.py:39
  34.8 0.0 copy-start.1
  34.8 0.0 copy-start
  34.8 0.0 all-gather.4.cloned.1.call-start
  34.9 24.7 %copy.22 = bf16[4608,2000]{1,0:T(8,128)(2,1)} copy(bf16[4608,2000]{0,1:T(8,128)(2,1)} %param.7) | data formatting | bytes 36864000 | tf_op args[2]
  59.6 0.0 copy-done.1
  59.6 0.2 fusion.12
  59.8 0.2 copy.33
  60.0 0.0 copy-done
  60.0 98.8 %all-to-all-done.1 = bf16[128,1,64,576]{3,2,1,0:T(8,128)(2,1)} async-done(((bf16[128,1,64,576]{3,2,1,0:T(8,128)(2,1)}), bf16[128,1,64,576]{3,2,1,0:T(8,128)(2,1)}, u32[]{:S(2)}, u32[]{:S(2)}) %all-to-all-start.1) | async-done | bytes 9437216 | tf_op jit(solution)/shard_map/all_to_all | solution.py:39
  158.8 27.7 %fusion.5 = (f32[1024]{0:T(1024)S(1)}, f32[1024,2000,1]{0,1,2:T(8,128)S(1)}) fusion(bf16[1024,576,8]{1,0,2:T(8,128)(2,1)} %bitcast.3, bf16[8,576,2000]{2,1,0:T(8,128)(2,1)} %bitcast.34), kind=kOutput, calls=%fused_computation.7 | convolution fusion | flops 18880512000 | bytes 36065280 | tf_op jit(solution)/shard_map/vgrd,vdc->grc/dot_general | solution.py:50
  186.5 9.4 %multiply_reduce_fusion = f32[1024,16]{0,1:T(8,128)} fusion(f32[1024,32]{0,1:T(8,128)S(1)} %copy.33, s32[32,16]{0,1:T(8,128)S(1)} %broadcast_subtract_fusion, f32[1024,2000,1]{0,1,2:T(8,128)S(1)} %get-tuple-element.3), kind=kOutput, calls=%fused_computation.11 | convolution fusion | flops 12589064192 | bytes 8390656 | tf_op jit(solution)/shard_map/dot_general | solution.py:64
  195.9 0.0 all-gather.4.cloned.1.call-update
  195.9 71.2 %all-gather.1 = f32[131072]{0:T(1024)S(1)} all-gather(f32[1024]{0:T(1024)S(1)} %get-tuple-element.2), channel_id=3, replica_groups=mesh['vocab'=8,'sample'=4,'prompt'=4] {'vocab','sample','prompt'}, dimensions={0}, use_global_device_ids=true | all-gather | bytes 528384 | tf_op jit(solution)/shard_map/all_gather | solution.py:22
  267.1 0.1 reshape.39
  267.3 0.6 dynamic_slice.7
  267.9 15.5 %all-gather.4.cloned.1.call-done = f32[131072,16]{0,1:T(8,128)} async-done(((f32[1024,16]{0,1:T(8,128)}), f32[131072,16]{0,1:T(8,128)}) %all-gather.4.cloned.1.call-update) | async-done | bytes 8388624 | tf_op jit(solution)/shard_map/all_gather | solution.py:22
  283.4 8.2 %copy.35 = f32[2,8,128,1024]{3,2,1,0:T(8,128)S(1)} copy(f32[2,8,128,1024]{3,1,2,0:T(8,128)} %bitcast.35) | data formatting | bytes 16777216
  291.6 1.1 bitcast_reduce_fusion
  292.7 1.0 convolution_log_fusion
  (5 shorter events, 0.1 us)
Async XLA Ops:
  8.8 11.3 %all-to-all-start = ((f32[8,1,64]{2,1,0:T(1,128)}), f32[8,1,64]{2,1,0:T(1,128)S(1)}, u32[]{:S(2)}, u32[]{:S(2)}) async-start(f32[8,1,64]{2,1,0:T(1,128)} %broadcast_in_dim.2), calls=%async_computation | async-start | bytes 8192 | tf_op jit(solution)/shard_map/all_to_all | solution.py:12
  26.6 132.2 %all-to-all-start.1 = ((bf16[128,1,64,576]{3,2,1,0:T(8,128)(2,1)}), bf16[128,1,64,576]{3,2,1,0:T(8,128)(2,1)}, u32[]{:S(2)}, u32[]{:S(2)}) async-start(bf16[128,1,64,576]{3,2,1,0:T(8,128)(2,1)} %stack.3), calls=%async_computation.1 | async-start | bytes 20971520 | tf_op jit(solution)/shard_map/all_to_all | solution.py:39
  34.8 24.8 %copy-start.1 = (s32[1024]{0:T(1024)S(1)}, s32[1024]{0:T(1024)}, u32[]{:S(2)}) copy-start(s32[1024]{0:T(1024)} %param.9) | copy-start | bytes 12292
  34.8 25.2 %copy-start = (s32[32,16]{0,1:T(8,128)S(1)}, s32[32,16]{0,1:T(8,128)}, u32[]{:S(2)}) copy-start(s32[32,16]{0,1:T(8,128)} %param.8) | copy-start | bytes 6148
  34.8 248.6 %all-gather.4.cloned.1.call-start = ((), (), s32[]{:S(2)}) async-start(), calls=%async_computation.2 | async-start | bytes 8454144 | tf_op jit(solution)/shard_map/all_gather | solution.py:22
Sparse Core Ops, SparseCore 0:
  196.0 87.3 all-gather.3
